TPU v7x, 128 devices: a whole 4x4x4 slice. The times are simulated.
128 devices in a mesh: aa: 16 (over x, z_hi, core), ba: 8 (over y, z_lo).
Axes of the slice: x: 4, y: 4, z: 4 (z_hi: 2, z_lo: 2; z = z_hi * 2 + z_lo), core: 2. Of those that a mesh axis runs over, the one named last changes fastest.
Arguments:
- amplitudes: bfloat16 [2048, 2048], P('aa', 'ba'), may hold values from -6 to 6
- code: int32 [32, 2048], replicated, may hold values from -2048 to 2048, as said below
- counts: int32 [128], replicated, may hold values from 1 to 16, as said below
- pair_irrep: int32 [32], replicated, may hold values from 0 to 7
- integrals: bfloat16 [32, 32], replicated, may hold values from -3 to 3
- one_body: bfloat16 [32], replicated, may hold values from -1.5 to 1.5
Outputs:
- sigma: bfloat16 [2048, 2048], P('aa', 'ba')
Inputs may be any that keep to these rules, and one draw needn't show every extreme that they name: |code| - 1 names the target string of a replacement and the sign of code its sign; some entries reach both ends. `counts`: the live strings of fine block j fill its first slots, from slot j * 16 on; in every draw some block is full and some holds one string.
All inputs are finite; a program needn't handle non-finite values.
Results may differ from a plain program's by a relative error of at most 0.0045.
Values may be sent and summed in bfloat16 or wider, within the bound.
A program may use at most 128 MiB of HBM per device.

v0:
```python
import jax
import jax.numpy as jnp
from jax import lax
from jax.sharding import PartitionSpec as P


def one_hot(tables, signs, first, width):
    ids = first + jnp.arange(width, dtype=jnp.int32)
    return jnp.where(
        tables[:, :, None] == ids[None, None, :], signs[:, :, None], jnp.zeros((), jnp.bfloat16)
    )


def alpha_term(tables, signs, values, start_a, rows_a, rows_b, count):
    groups = tables.shape[0] // 8
    rows_t = tables.reshape(groups, 8, count)
    rows_s = signs.reshape(groups, 8, count)

    def one_group(carry, items):
        tab, sgn, val = items
        hot = one_hot(tab, sgn, start_a, rows_a)
        return (
            carry + jnp.einsum("prk,pkb->rb", hot, val, preferred_element_type=jnp.float32),
            None,
        )

    total, _ = lax.scan(
        one_group,
        jnp.zeros((count, rows_b), jnp.float32),
        (rows_t, rows_s, values.reshape(groups, 8, rows_a, rows_b)),
    )
    return total


def per_device(amplitudes, code, counts, pair_irrep, integrals, one_body):
    rows_a, rows_b = amplitudes.shape
    pairs, strings = code.shape
    groups = pairs // 8
    capacity = strings // counts.shape[0]
    slots = jnp.arange(strings, dtype=jnp.int32)
    live_all = (slots % capacity < jnp.repeat(counts, capacity)).astype(jnp.bfloat16)
    start_a = lax.axis_index("aa") * rows_a
    start_b = lax.axis_index("ba") * rows_b
    live_a = lax.dynamic_slice_in_dim(live_all, start_a, rows_a)
    live_b = lax.dynamic_slice_in_dim(live_all, start_b, rows_b)
    masked = amplitudes * (live_a[:, None] * live_b[None, :])
    target = jnp.abs(code) - 1
    signs = jnp.sign(code).astype(jnp.bfloat16)
    target_a = lax.dynamic_slice_in_dim(target, start_a, rows_a, 1).reshape(groups, 8, rows_a)
    signs_a = lax.dynamic_slice_in_dim(signs, start_a, rows_a, 1).reshape(groups, 8, rows_a)
    target_b = lax.dynamic_slice_in_dim(target, start_b, rows_b, 1).reshape(groups, 8, rows_b)
    signs_b = lax.dynamic_slice_in_dim(signs, start_b, rows_b, 1).reshape(groups, 8, rows_b)
    piece = lax.all_gather(masked, "ba", axis=1, tiled=True)
    start = jnp.int32(0)

    def one_group(items):
        tab, sgn = items
        hot = one_hot(tab, sgn, start, piece.shape[1])
        return jnp.einsum("pkc,ic->pik", hot, piece, preferred_element_type=jnp.float32)

    beta_sum = lax.map(one_group, (target_b, signs_b)).reshape(pairs, rows_a, rows_b)
    dbeta = (beta_sum * live_b[None, None, :]).astype(jnp.bfloat16)
    alpha_piece = lax.all_gather(masked, "aa", axis=0, tiled=True)
    alpha_start = jnp.int32(0)

    def one_group(items):
        tab, sgn = items
        hot = one_hot(tab, sgn, alpha_start, alpha_piece.shape[0])
        return jnp.einsum("pkj,jb->pkb", hot, alpha_piece, preferred_element_type=jnp.float32)

    alpha_sum = lax.map(one_group, (target_a, signs_a)).reshape(pairs, rows_a, rows_b)
    dalpha = (alpha_sum * live_a[None, :, None]).astype(jnp.bfloat16)
    weights = jnp.where(
        pair_irrep[:, None] == pair_irrep[None, :], integrals, jnp.zeros((), jnp.bfloat16)
    )
    gbeta_full = jnp.einsum("pq,qik->pik", weights, dbeta, preferred_element_type=jnp.float32)
    galpha_full = jnp.einsum("pq,qik->pik", weights, dalpha, preferred_element_type=jnp.float32)
    gbeta = gbeta_full.astype(jnp.bfloat16)
    combined = (gbeta_full + 0.5 * galpha_full).astype(jnp.bfloat16)
    local = jnp.einsum("p,pik->ik", one_body, dbeta, preferred_element_type=jnp.float32)
    local = local + jnp.einsum("p,pik->ik", one_body, dalpha, preferred_element_type=jnp.float32)
    half_beta = gbeta * 0.5
    gathered_piece = lax.all_gather(half_beta, "ba", axis=2, tiled=True)
    gathered_start = jnp.int32(0)
    width = gathered_piece.shape[2]

    def one_group(acc, items):
        tab, sgn, val = items
        hot = one_hot(tab, sgn, gathered_start, width)
        return (acc + jnp.einsum("pbk,pak->ab", hot, val, preferred_element_type=jnp.float32), None)

    total, _ = lax.scan(
        one_group,
        jnp.zeros((rows_a, rows_b), jnp.float32),
        (target_b, signs_b, gathered_piece.reshape(groups, 8, rows_a, width)),
    )
    beta_part = total
    alpha_rows = lax.psum_scatter(
        alpha_term(target, signs, combined, start_a, rows_a, rows_b, lax.axis_size("aa") * rows_a),
        "aa",
        scatter_dimension=0,
        tiled=True,
    )
    total = local + beta_part + alpha_rows
    return (total * (live_a[:, None] * live_b[None, :])).astype(jnp.bfloat16)


def solution(mesh):
    placed = (P("aa", "ba"), P(), P(), P(), P(), P())
    return jax.shard_map(
        per_device, mesh=mesh, in_specs=placed, out_specs=P("aa", "ba"), check_vma=False
    )
```

profile of v0, /device:TPU:0, one launch (start us, length us, event | category | flops | bytes accessed | tf_op | source)
XLA Modules:
  0.0 478.1 jit_solution(13989300065784865499)
XLA Ops:
  9.2 29.7 %all_gather.9 = bf16[128,2048]{1,0:T(8,128)(2,1)S(1)} all-gather(bf16[128,256]{1,0:T(8,128)(2,1)} %multiply_multiply_fusion), channel_id=1, replica_groups=mesh['aa'=16,'ba'=8] {'ba'}, dimensions={1}, use_global_device_ids=true | all-gather | bytes 589824 | tf_op jit(solution)/shard_map/all_gather | solution.py:53
  40.0 13.7 %while.42 = (s32[]{:T(128)}, f32[4,8,128,256]{2,3,1,0:T(8,128)}, s32[4,8,256]{2,1,0:T(8,128)S(1)}, bf16[4,8,256]{2,1,0:T(8,128)(2,1)S(1)}, bf16[128,2048]{1,0:T(8,128)(2,1)S(1)}, /*index=5*/s32[]{:T(128)}) while((s32[]{:T(128)}, f32[4,8,128,256]{2,3,1,0:T(8,128)}, s32[4,8,256]{2,1,0:T(8,128)S(1)}, bf16[4,8,256]{2,1,0:T(8,128)(2,1)S(1)}, ...), condition=%wide.region_1.2_spmd, body=%wide.region_0.1_spmd.sunk | while | flops 1082130432 | bytes 1609817 | solution.py:61
  40.0 3.4 fusion.91
  43.4 3.4 fusion.91
  46.9 3.4 fusion.91
  50.3 3.4 fusion.91
  53.7 5.5 %copy.13 = f32[32,128,256]{2,0,1:T(8,128)} copy(f32[32,128,256]{1,2,0:T(8,128)} %bitcast.130) | data formatting | bytes 8388608 | tf_op jit(solution)/shard_map/reshape | solution.py:61
  59.2 5.5 %convert_multiply_fusion = (bf16[32,128,256]{2,0,1:T(8,128)(2,1)}, f32[32,128,256]{2,0,1:T(8,128)}) fusion(f32[32,128,256]{2,0,1:T(8,128)} %copy.13, f32[256]{0:T(256)S(1)} %get-tuple-element.237, bf16[32,32]{1,0:T(8,128)(2,1)S(1)} %copy-done.2, s32[32]{0:T(128)S(1)} %copy-done.3), kind=kOutput, calls=%fused_computation.55 | convolution fusion | flops 71305216 | bytes 10488960 | tf_op jit(solution)/shard_map/pq,qik->pik/dot_general | solution.py:76
  64.9 2.6 fusion.52
  67.5 14.2 %while.43 = (s32[]{:T(128)}, f32[4,8,128,256]{3,2,1,0:T(8,128)}, s32[4,8,128]{2,1,0:T(8,128)S(1)}, bf16[4,8,128]{2,1,0:T(8,128)(2,1)S(1)}, bf16[2048,256]{1,0:T(8,128)(2,1)}, /*index=5*/s32[]{:T(128)}) while((s32[]{:T(128)}, f32[4,8,128,256]{3,2,1,0:T(8,128)}, s32[4,8,128]{2,1,0:T(8,128)S(1)}, bf16[4,8,128]{2,1,0:T(8,128)(2,1)S(1)}, ...), condition=%wide.region_3.4_spmd, body=%wide.region_2.3_spmd.sunk | while | flops 1077936128 | bytes 2115673 | solution.py:71
  67.6 3.6 fusion.94
  71.2 3.5 fusion.94
  74.7 3.5 fusion.94
  78.2 3.5 fusion.94
  81.7 4.8 %fusion.65 = f32[1,128,256]{2,0,1:T(1,128)S(1)} fusion(bf16[32]{0:T(256)(128)(2,1)S(1)} %copy-done, f32[32,128,256]{2,1,0:T(8,128)} %bitcast.128, f32[128]{0:T(128)S(1)} %get-tuple-element.235), kind=kOutput, calls=%fused_computation.80 | convolution fusion | flops 4194304 | bytes 4325952 | tf_op jit(solution)/shard_map/p,pik->ik/dot_general | solution.py:81
  86.5 4.9 %fusion.50 = bf16[4,8,128,256]{3,1,0,2:T(8,128)(2,1)S(1)} fusion(f32[32,128,256]{2,0,1:T(8,128)S(1)} %copy-done.1, bf16[32,32]{1,0:T(8,128)(2,1)S(1)} %copy-done.2, s32[32]{0:T(128)S(1)} %copy-done.3, f32[32,128,256]{2,1,0:T(8,128)} %bitcast.129, f32[128]{0:T(128)S(1)} %get-tuple-element.235), kind=kOutput, calls=%fused_computation.56 | convolution fusion | flops 72353792 | bytes 10488448 | tf_op jit(solution)/shard_map/pq,qik->pik/dot_general | solution.py:77
  91.4 27.8 %while.45 = (s32[]{:T(128)}, f32[2048,256]{1,0:T(8,128)}, s32[4,8,2048]{2,1,0:T(8,128)S(1)}, s32[]{:T(128)}, bf16[4,8,2048]{2,1,0:T(8,128)(2,1)S(1)}, /*index=5*...) while((s32[]{:T(128)}, f32[2048,256]{1,0:T(8,128)}, s32[4,8,2048]{2,1,0:T(8,128)S(1)}, ...), condition=%wide.region_7.8_spmd.clone, body=%wide.region_6.7_spmd.clone.sunk | while | flops 1078984832 | bytes 6063223 | solution.py:27
  91.6 6.1 %fusion.98 = f32[2048,256]{1,0:T(8,128)} fusion(s32[128]{0:T(128)S(1)} %iota_add_fusion.2, s32[8,2048]{1,0:T(8,128)S(1)} %dynamic-slice_bitcast_fusion.26, f32[2048,256]{1,0:T(8,128)} %get-tuple-element.419, bf16[8,2048]{1,0:T(8,128)(2,1)S(1)} %dynamic-slice_bitcast_fusion.27, pred[]{:T(512)S(6)} %compare.8, ...), kind=kOutput, calls=%fused_computation.42.clone.1 | convolution fusion | flops 1078984704 | bytes 4817409 | tf_op jit(solution)/shard_map/while/body/eval_jaxpr/prk,pkb->rb/dot_general | solution.py:23
  97.8 7.1 %fusion.98 = f32[2048,256]{1,0:T(8,128)} fusion(s32[128]{0:T(128)S(1)} %iota_add_fusion.2, s32[8,2048]{1,0:T(8,128)S(1)} %dynamic-slice_bitcast_fusion.26, f32[2048,256]{1,0:T(8,128)} %get-tuple-element.419, bf16[8,2048]{1,0:T(8,128)(2,1)S(1)} %dynamic-slice_bitcast_fusion.27, pred[]{:T(512)S(6)} %compare.8, ...), kind=kOutput, calls=%fused_computation.42.clone.1 | convolution fusion | flops 1078984704 | bytes 4817409 | tf_op jit(solution)/shard_map/while/body/eval_jaxpr/prk,pkb->rb/dot_general | solution.py:23
  104.9 7.1 %fusion.98 = f32[2048,256]{1,0:T(8,128)} fusion(s32[128]{0:T(128)S(1)} %iota_add_fusion.2, s32[8,2048]{1,0:T(8,128)S(1)} %dynamic-slice_bitcast_fusion.26, f32[2048,256]{1,0:T(8,128)} %get-tuple-element.419, bf16[8,2048]{1,0:T(8,128)(2,1)S(1)} %dynamic-slice_bitcast_fusion.27, pred[]{:T(512)S(6)} %compare.8, ...), kind=kOutput, calls=%fused_computation.42.clone.1 | convolution fusion | flops 1078984704 | bytes 4817409 | tf_op jit(solution)/shard_map/while/body/eval_jaxpr/prk,pkb->rb/dot_general | solution.py:23
  112.1 7.1 %fusion.98 = f32[2048,256]{1,0:T(8,128)} fusion(s32[128]{0:T(128)S(1)} %iota_add_fusion.2, s32[8,2048]{1,0:T(8,128)S(1)} %dynamic-slice_bitcast_fusion.26, f32[2048,256]{1,0:T(8,128)} %get-tuple-element.419, bf16[8,2048]{1,0:T(8,128)(2,1)S(1)} %dynamic-slice_bitcast_fusion.27, pred[]{:T(512)S(6)} %compare.8, ...), kind=kOutput, calls=%fused_computation.42.clone.1 | convolution fusion | flops 1078984704 | bytes 4817409 | tf_op jit(solution)/shard_map/while/body/eval_jaxpr/prk,pkb->rb/dot_general | solution.py:23
  119.2 274.2 %all-gather.5.cloned.1.call-done = bf16[32,128,2048]{2,0,1:T(8,128)(2,1)} async-done(((bf16[32,128,256]{2,0,1:T(8,128)(2,1)}), bf16[32,128,2048]{2,0,1:T(8,128)(2,1)}) %all-gather.5.cloned.1.call-update) | async-done | bytes 16777232 | tf_op jit(solution)/shard_map/all_gather | solution.py:83
  393.4 40.3 %while.44 = (s32[]{:T(128)}, f32[128,256]{1,0:T(8,128)S(1)}, bf16[4,8,128,2048]{3,1,0,2:T(8,128)(2,1)}, s32[4,8,256]{2,1,0:T(8,128)S(1)}, bf16[4,8,256]{2,1,0:T(8,128)(2,1)S(1)}, /*index=5*/s32[]{:T(128)}, s32[]{:T(128)}) while((s32[]{:T(128)}, f32[128,256]{1,0:T(8,128)S(1)}, bf16[4,8,128,2048]{3,1,0,2:T(8,128)(2,1)}, ...), condition=%wide.region_5.6_spmd.clone, body=%wide.region_4.5_spmd.clone.sunk | while | flops 1082195968 | bytes 29659240 | solution.py:92
  393.4 2.5 constant_dynamic-slice_fusion.4
  397.9 5.5 %fusion.97 = f32[128,256]{1,0:T(8,128)S(1)} fusion(bf16[1,8,128,2048]{3,1,0,2:T(8,128)(2,1)S(1)} %constant_dynamic-slice_fusion.4, f32[128,256]{1,0:T(8,128)S(1)} %get-tuple-element.442, pred[]{:T(512)S(6)} %compare.7, bf16[8,256,2048]{2,1,0:T(8,128)(2,1)S(1)} %fusion.96), kind=kOutput, calls=%fused_computation.32.clone.2 | convolution fusion | flops 1073807360 | bytes 12845057 | tf_op jit(solution)/shard_map/while/body/eval_jaxpr/pbk,pak->ab/dot_general | solution.py:90
  403.5 2.5 constant_dynamic-slice_fusion.4
  408.0 5.5 %fusion.97 = f32[128,256]{1,0:T(8,128)S(1)} fusion(bf16[1,8,128,2048]{3,1,0,2:T(8,128)(2,1)S(1)} %constant_dynamic-slice_fusion.4, f32[128,256]{1,0:T(8,128)S(1)} %get-tuple-element.442, pred[]{:T(512)S(6)} %compare.7, bf16[8,256,2048]{2,1,0:T(8,128)(2,1)S(1)} %fusion.96), kind=kOutput, calls=%fused_computation.32.clone.2 | convolution fusion | flops 1073807360 | bytes 12845057 | tf_op jit(solution)/shard_map/while/body/eval_jaxpr/pbk,pak->ab/dot_general | solution.py:90
  413.6 2.6 constant_dynamic-slice_fusion.4
  418.2 5.5 %fusion.97 = f32[128,256]{1,0:T(8,128)S(1)} fusion(bf16[1,8,128,2048]{3,1,0,2:T(8,128)(2,1)S(1)} %constant_dynamic-slice_fusion.4, f32[128,256]{1,0:T(8,128)S(1)} %get-tuple-element.442, pred[]{:T(512)S(6)} %compare.7, bf16[8,256,2048]{2,1,0:T(8,128)(2,1)S(1)} %fusion.96), kind=kOutput, calls=%fused_computation.32.clone.2 | convolution fusion | flops 1073807360 | bytes 12845057 | tf_op jit(solution)/shard_map/while/body/eval_jaxpr/pbk,pak->ab/dot_general | solution.py:90
  423.7 2.5 constant_dynamic-slice_fusion.4
  428.2 5.5 %fusion.97 = f32[128,256]{1,0:T(8,128)S(1)} fusion(bf16[1,8,128,2048]{3,1,0,2:T(8,128)(2,1)S(1)} %constant_dynamic-slice_fusion.4, f32[128,256]{1,0:T(8,128)S(1)} %get-tuple-element.442, pred[]{:T(512)S(6)} %compare.7, bf16[8,256,2048]{2,1,0:T(8,128)(2,1)S(1)} %fusion.96), kind=kOutput, calls=%fused_computation.32.clone.2 | convolution fusion | flops 1073807360 | bytes 12845057 | tf_op jit(solution)/shard_map/while/body/eval_jaxpr/pbk,pak->ab/dot_general | solution.py:90
  433.8 36.2 %reduce-scatter.2.cloned.1.call-done = f32[128,256]{1,0:T(8,128)} async-done(((f32[2048,256]{1,0:T(8,128)}), f32[128,256]{1,0:T(8,128)}) %reduce-scatter.2.cloned.1.call-update) | async-done | bytes 131088 | tf_op jit(solution)/shard_map/reduce_scatter | solution.py:98
  (75 shorter events, 13.9 us)
Async XLA Ops:
  6.5 58.4 %copy-start = (bf16[32]{0:T(256)(128)(2,1)S(1)}, bf16[32]{0:T(256)(128)(2,1)}, u32[]{:S(2)}) copy-start(bf16[32]{0:T(256)(128)(2,1)} %param.19) | copy-start | bytes 196
  6.5 61.0 %all-gather.3.cloned.1.call-start = ((), (), s32[]{:S(2)}) async-start(), calls=%async_computation.1 | async-start | bytes 1114112 | tf_op jit(solution)/shard_map/all_gather | solution.py:63
  9.1 384.3 %all-gather.5.cloned.1.call-start = ((), (), s32[]{:S(2)}) async-start(), calls=%async_computation.2 | async-start | bytes 18874368 | tf_op jit(solution)/shard_map/all_gather | solution.py:83
  53.7 5.5 %copy-start.2 = (bf16[32,32]{1,0:T(8,128)(2,1)S(1)}, bf16[32,32]{1,0:T(8,128)(2,1)}, u32[]{:S(2)}) copy-start(bf16[32,32]{1,0:T(8,128)(2,1)} %param.18) | copy-start | bytes 6148
  53.7 5.5 %copy-start.3 = (s32[32]{0:T(128)S(1)}, s32[32]{0:T(128)}, u32[]{:S(2)}) copy-start(s32[32]{0:T(128)} %param.17) | copy-start | bytes 388
  64.8 405.2 %reduce-scatter.2.cloned.1.call-start = ((), (), s32[]{:S(2)}) async-start(), calls=%async_computation.3 | async-start | bytes 2228224 | tf_op jit(solution)/shard_map/reduce_scatter | solution.py:98
  81.7 4.8 %copy-start.1 = (f32[32,128,256]{2,0,1:T(8,128)S(1)}, f32[32,128,256]{2,0,1:T(8,128)}, u32[]{:S(2)}) copy-start(f32[32,128,256]{2,0,1:T(8,128)} %get-tuple-element.243) | copy-start | bytes 12582916
Sparse Core Ops, SparseCore 0:
  9.7 47.5 all-gather.2
  64.9 328.4 all-gather.4
  397.4 72.5 reduce-scatter.1
where the time goes:
time: 479 us; the launch traced here: 478 us
  waiting for transfers between devices  310 us (65%)
  matrix products  94.9 us (20%)
  blocking collectives  29.7 us (6%)
  local copies, waits for them, and re-layouts  17 us (4%)
  between operations  13.2 us (3%)
  other arithmetic  12.3 us (3%)
    all_gather x1, waiting for transfers between devices, per_device(): gathered_piece = lax.all_gather(half_beta, 'ba', axis=2, tiled=True)  274 us
    reduce_scatter x1, waiting for transfers between devices, per_device(): lax.psum_scatter(alpha_term(target, signs, combined, start_a, rows_a, row...  36.2 us
    all_gather x1, blocking collectives, per_device(): piece = lax.all_gather(masked, 'ba', axis=1, tiled=True)  29.7 us
    dot_general x4, matrix products, one_group(): jnp.einsum('prk,pkb->rb', hot, val, preferred_element_type=jnp.float32)  27.3 us
    dot_general x4, matrix products, one_group(): jnp.einsum('pbk,pak->ab', hot, val, preferred_element_type=jnp.float32)  22 us
    dot_general x4, matrix products, one_group(): jnp.einsum('pkj,jb->pkb', hot, alpha_piece, preferred_element_type=jnp.fl...  14.1 us
    dot_general x4, matrix products, one_group(): jnp.einsum('pkc,ic->pik', hot, piece, preferred_element_type=jnp.float32)  13.7 us
    dynamic_slice x4, local copies, waits for them, and re-layouts, per_device(): lax.scan(one_group, jnp.zeros((rows_a, rows_b), jnp.float32), (target_b,...  10.1 us
  transfers between devices with their start and end apart: 3, of which 2 were waited for; matrix products, arithmetic and copies ran while one was open for 25% of the time, Pallas kernels for 0%

commit v1 on v0

--- a/solution.py
+++ b/solution.py
@@ -80,7 +80,9 @@
     local = jnp.einsum("p,pik->ik", one_body, dbeta, preferred_element_type=jnp.float32)
     local = local + jnp.einsum("p,pik->ik", one_body, dalpha, preferred_element_type=jnp.float32)
     half_beta = gbeta * 0.5
-    gathered_piece = lax.all_gather(half_beta, "ba", axis=2, tiled=True)
+    gathered_piece = jnp.concatenate(
+        lax.all_to_all(jnp.stack([half_beta] * lax.axis_size("ba")), "ba", 0, 0), axis=2
+    )
     gathered_start = jnp.int32(0)
     width = gathered_piece.shape[2]
 

time: 479 us -> 392 us (0.82)
  waiting for transfers between devices: 310 us -> 205 us
  local copies, waits for them, and re-layouts: 17 us -> 46.8 us
  matrix products: 94.9 us -> 85.5 us
  other arithmetic: 12.3 us -> 3.76 us
  starting transfers between devices: 0.09 us -> 6.01 us
    all_gather x1 -> x0, waiting for transfers between devices: 274 us -> none  [per_device(): gathered_piece = lax.all_gather(half_beta, 'ba', axis=2, tiled=True)]
    all_gather x1, waiting for transfers between devices: 0.02 us -> 119 us  [per_device(): alpha_piece = lax.all_gather(masked, 'aa', axis=0, tiled=True)]
    all_to_all x0 -> x1, waiting for transfers between devices: none -> 48 us  [per_device(): lax.all_to_all(jnp.stack([half_beta] * lax.axis_size('ba')), 'ba', 0, 0)]
    all_to_all x0 -> x1, local copies, waits for them, and re-layouts: none -> 22.6 us  [per_device(): lax.all_to_all(jnp.stack([half_beta] * lax.axis_size('ba')), 'ba', 0, 0)]
    dot_general x0 -> x4, local copies, waits for them, and re-layouts: none -> 10.2 us  [one_group(): jnp.einsum('pbk,pak->ab', hot, val, preferred_element_type=jnp.float32)]
    dynamic_slice x4 -> x0, local copies, waits for them, and re-layouts: 10.1 us -> none  [per_device(): lax.scan(one_group, jnp.zeros((rows_a, rows_b), jnp.float32), (target_b,...]
    dot_general x4, matrix products: 22 us -> 12.6 us  [one_group(): jnp.einsum('pbk,pak->ab', hot, val, preferred_element_type=jnp.float32)]
    dot_general x4 -> x0, other arithmetic: 7.93 us -> none  [one_group(): jnp.einsum('pbk,pak->ab', hot, val, preferred_element_type=jnp.float32)]
  transfers between devices with their start and end apart: 3 -> 3, of which waited for: 2 -> 3; matrix products, arithmetic and copies ran while one was open for 25% -> 26% of each run, Pallas kernels for 0% -> 0%
where the time goes in v1:
time: 392 us; the launch traced here: 390 us
  waiting for transfers between devices  205 us (52%)
  matrix products  85.5 us (22%)
  local copies, waits for them, and re-layouts  46.8 us (12%)
  blocking collectives  29.6 us (8%)
  between operations  13.5 us (3%)
  starting transfers between devices  6.01 us (2%)
    all_gather x1, waiting for transfers between devices, per_device(): alpha_piece = lax.all_gather(masked, 'aa', axis=0, tiled=True)  119 us
    all_to_all x1, waiting for transfers between devices, per_device(): lax.all_to_all(jnp.stack([half_beta] * lax.axis_size('ba')), 'ba', 0, 0)  48 us
    reduce_scatter x1, waiting for transfers between devices, per_device(): lax.psum_scatter(alpha_term(target, signs, combined, start_a, rows_a, row...  37.4 us
    all_gather x1, blocking collectives, per_device(): piece = lax.all_gather(masked, 'ba', axis=1, tiled=True)  29.6 us
    dot_general x4, matrix products, one_group(): jnp.einsum('prk,pkb->rb', hot, val, preferred_element_type=jnp.float32)  27.1 us
    all_to_all x1, local copies, waits for them, and re-layouts, per_device(): lax.all_to_all(jnp.stack([half_beta] * lax.axis_size('ba')), 'ba', 0, 0)  22.6 us
    dot_general x4, matrix products, one_group(): jnp.einsum('pkj,jb->pkb', hot, alpha_piece, preferred_element_type=jnp.fl...  14 us
    dot_general x4, matrix products, one_group(): jnp.einsum('pkc,ic->pik', hot, piece, preferred_element_type=jnp.float32)  13.6 us
  transfers between devices with their start and end apart: 3, of which 3 were waited for; matrix products, arithmetic and copies ran while one was open for 26% of the time, Pallas kernels for 0%

profile of v1, /device:TPU:0, one launch (start us, length us, event | category | flops | bytes accessed | tf_op | source)
XLA Modules:
  0.0 390.3 jit_solution(12162741424288155000)
XLA Ops:
  8.5 29.6 %all_gather.6 = bf16[128,2048]{1,0:T(8,128)(2,1)S(1)} all-gather(bf16[128,256]{1,0:T(8,128)(2,1)S(1)} %multiply_multiply_fusion), channel_id=1, replica_groups=mesh['aa'=16,'ba'=8] {'ba'}, dimensions={1}, use_global_device_ids=true | all-gather | bytes 589824 | tf_op jit(solution)/shard_map/all_gather | solution.py:53
  39.2 13.7 %while.42 = (s32[]{:T(128)}, f32[4,8,128,256]{2,3,1,0:T(8,128)}, s32[4,8,256]{2,1,0:T(8,128)S(1)}, bf16[4,8,256]{2,1,0:T(8,128)(2,1)S(1)}, bf16[128,2048]{1,0:T(8,128)(2,1)S(1)}, /*index=5*/s32[]{:T(128)}) while((s32[]{:T(128)}, f32[4,8,128,256]{2,3,1,0:T(8,128)}, s32[4,8,256]{2,1,0:T(8,128)S(1)}, bf16[4,8,256]{2,1,0:T(8,128)(2,1)S(1)}, ...), condition=%wide.region_1.2_spmd, body=%wide.region_0.1_spmd.sunk | while | flops 1082130432 | bytes 1609817 | solution.py:61
  39.3 3.4 fusion.103
  42.7 3.4 fusion.103
  46.1 3.4 fusion.103
  49.5 3.4 fusion.103
  52.9 5.5 %copy.23 = f32[32,128,256]{2,0,1:T(8,128)} copy(f32[32,128,256]{1,2,0:T(8,128)} %bitcast.137) | data formatting | bytes 8388608 | tf_op jit(solution)/shard_map/reshape | solution.py:61
  58.4 5.0 %convert_multiply_fusion = (bf16[32,128,256]{2,0,1:T(8,128)(2,1)S(1)}, f32[32,128,256]{2,0,1:T(8,128)}) fusion(f32[32,128,256]{2,0,1:T(8,128)} %copy.23, f32[256]{0:T(256)S(1)} %get-tuple-element.254, bf16[32,32]{1,0:T(8,128)(2,1)S(1)} %copy-done.2, s32[32]{0:T(128)S(1)} %copy-done.3), kind=kOutput, calls=%fused_computation.56 | convolution fusion | flops 71305216 | bytes 10488960 | tf_op jit(solution)/shard_map/pq,qik->pik/dot_general | solution.py:76
  64.6 6.0 %stack.2 = bf16[8,32,128,256]{3,2,1,0:T(8,128)(2,1)} broadcast(bf16[32,128,256]{2,1,0:T(8,128)(2,1)S(1)} %copy.25), dimensions={1,2,3} | broadcast | bytes 18874368 | tf_op jit(solution)/shard_map/stack | solution.py:84
  70.6 5.7 %all-to-all-start = ((bf16[8,32,128,256]{3,2,1,0:T(8,128)(2,1)}), bf16[8,32,128,256]{3,2,1,0:T(8,128)(2,1)}, u32[]{:S(2)}, u32[]{:S(2)}) async-start(bf16[8,32,128,256]{3,2,1,0:T(8,128)(2,1)} %stack.2), calls=%async_computation | async-start | bytes 33554432 | tf_op jit(solution)/shard_map/all_to_all | solution.py:84
  80.0 118.6 %all-gather.2.cloned.1.call-done = bf16[2048,256]{1,0:T(8,128)(2,1)} async-done(((bf16[128,256]{1,0:T(8,128)(2,1)}), bf16[2048,256]{1,0:T(8,128)(2,1)}) %all-gather.2.cloned.1.call-update) | async-done | bytes 1048592 | tf_op jit(solution)/shard_map/all_gather | solution.py:63
  198.6 14.0 %while.43 = (s32[]{:T(128)}, f32[4,8,128,256]{3,2,1,0:T(8,128)}, s32[4,8,128]{2,1,0:T(8,128)S(1)}, bf16[4,8,128]{2,1,0:T(8,128)(2,1)S(1)}, bf16[2048,256]{1,0:T(8,128)(2,1)}, /*index=5*/s32[]{:T(128)}) while((s32[]{:T(128)}, f32[4,8,128,256]{3,2,1,0:T(8,128)}, s32[4,8,128]{2,1,0:T(8,128)S(1)}, bf16[4,8,128]{2,1,0:T(8,128)(2,1)S(1)}, ...), condition=%wide.region_3.4_spmd, body=%wide.region_2.3_spmd.sunk | while | flops 1077936128 | bytes 2115673 | solution.py:71
  198.6 3.5 fusion.106
  202.1 3.6 fusion.106
  205.7 3.5 fusion.106
  209.1 3.5 fusion.106
  212.6 6.0 %fusion.57 = bf16[4,8,128,256]{3,1,0,2:T(8,128)(2,1)S(1)} fusion(f32[32,128,256]{2,0,1:T(8,128)} %get-tuple-element.260, bf16[32,32]{1,0:T(8,128)(2,1)S(1)} %copy-done.2, s32[32]{0:T(128)S(1)} %copy-done.3, f32[32,128,256]{2,1,0:T(8,128)} %bitcast.135, f32[128]{0:T(128)S(1)} %get-tuple-element.252), kind=kOutput, calls=%fused_computation.57 | convolution fusion | flops 72353792 | bytes 10488448 | tf_op jit(solution)/shard_map/pq,qik->pik/dot_general | solution.py:77
  218.6 27.6 %while.45 = (s32[]{:T(128)}, f32[2048,256]{1,0:T(8,128)}, s32[4,8,2048]{2,1,0:T(8,128)S(1)}, s32[]{:T(128)}, bf16[4,8,2048]{2,1,0:T(8,128)(2,1)S(1)}, /*index=5*...) while((s32[]{:T(128)}, f32[2048,256]{1,0:T(8,128)}, s32[4,8,2048]{2,1,0:T(8,128)S(1)}, ...), condition=%wide.region_7.8_spmd.clone, body=%wide.region_6.7_spmd.clone.sunk | while | flops 1078984832 | bytes 6063223 | solution.py:27
  218.8 6.0 %fusion.111 = f32[2048,256]{1,0:T(8,128)} fusion(s32[128]{0:T(128)S(1)} %iota_add_fusion.2, s32[8,2048]{1,0:T(8,128)S(1)} %dynamic-slice_bitcast_fusion.26, f32[2048,256]{1,0:T(8,128)} %get-tuple-element.436, bf16[8,2048]{1,0:T(8,128)(2,1)S(1)} %dynamic-slice_bitcast_fusion.27, pred[]{:T(512)S(6)} %compare.8, ...), kind=kOutput, calls=%fused_computation.43.clone.1 | convolution fusion | flops 1078984704 | bytes 4817409 | tf_op jit(solution)/shard_map/while/body/eval_jaxpr/prk,pkb->rb/dot_general | solution.py:23
  224.9 7.0 %fusion.111 = f32[2048,256]{1,0:T(8,128)} fusion(s32[128]{0:T(128)S(1)} %iota_add_fusion.2, s32[8,2048]{1,0:T(8,128)S(1)} %dynamic-slice_bitcast_fusion.26, f32[2048,256]{1,0:T(8,128)} %get-tuple-element.436, bf16[8,2048]{1,0:T(8,128)(2,1)S(1)} %dynamic-slice_bitcast_fusion.27, pred[]{:T(512)S(6)} %compare.8, ...), kind=kOutput, calls=%fused_computation.43.clone.1 | convolution fusion | flops 1078984704 | bytes 4817409 | tf_op jit(solution)/shard_map/while/body/eval_jaxpr/prk,pkb->rb/dot_general | solution.py:23
  232.1 7.0 %fusion.111 = f32[2048,256]{1,0:T(8,128)} fusion(s32[128]{0:T(128)S(1)} %iota_add_fusion.2, s32[8,2048]{1,0:T(8,128)S(1)} %dynamic-slice_bitcast_fusion.26, f32[2048,256]{1,0:T(8,128)} %get-tuple-element.436, bf16[8,2048]{1,0:T(8,128)(2,1)S(1)} %dynamic-slice_bitcast_fusion.27, pred[]{:T(512)S(6)} %compare.8, ...), kind=kOutput, calls=%fused_computation.43.clone.1 | convolution fusion | flops 1078984704 | bytes 4817409 | tf_op jit(solution)/shard_map/while/body/eval_jaxpr/prk,pkb->rb/dot_general | solution.py:23
  239.2 7.0 %fusion.111 = f32[2048,256]{1,0:T(8,128)} fusion(s32[128]{0:T(128)S(1)} %iota_add_fusion.2, s32[8,2048]{1,0:T(8,128)S(1)} %dynamic-slice_bitcast_fusion.26, f32[2048,256]{1,0:T(8,128)} %get-tuple-element.436, bf16[8,2048]{1,0:T(8,128)(2,1)S(1)} %dynamic-slice_bitcast_fusion.27, pred[]{:T(512)S(6)} %compare.8, ...), kind=kOutput, calls=%fused_computation.43.clone.1 | convolution fusion | flops 1078984704 | bytes 4817409 | tf_op jit(solution)/shard_map/while/body/eval_jaxpr/prk,pkb->rb/dot_general | solution.py:23
  246.2 4.6 %fusion.72 = f32[1,128,256]{2,0,1:T(1,128)S(1)} fusion(bf16[32]{0:T(256)(128)(2,1)S(1)} %copy-done, f32[32,128,256]{2,1,0:T(8,128)} %bitcast.136, f32[128]{0:T(128)S(1)} %get-tuple-element.252), kind=kOutput, calls=%fused_computation.81 | convolution fusion | flops 4194304 | bytes 4325952 | tf_op jit(solution)/shard_map/p,pik->ik/dot_general | solution.py:81
  250.8 48.0 %all-to-all-done = bf16[8,32,128,256]{3,2,1,0:T(8,128)(2,1)} async-done(((bf16[8,32,128,256]{3,2,1,0:T(8,128)(2,1)}), bf16[8,32,128,256]{3,2,1,0:T(8,128)(2,1)}, u32[]{:S(2)}, u32[]{:S(2)}) %all-to-all-start) | async-done | bytes 16777248 | tf_op jit(solution)/shard_map/all_to_all | solution.py:84
  298.9 22.6 %copy.26 = bf16[8,32,128,256]{2,3,0,1:T(8,128)(2,1)} copy(bf16[8,32,128,256]{3,2,1,0:T(8,128)(2,1)} %all-to-all-done) | data formatting | bytes 33554432 | tf_op jit(solution)/shard_map/all_to_all | solution.py:84
  321.4 23.0 %while.44 = (s32[]{:T(128)}, f32[128,256]{1,0:T(8,128)S(1)}, bf16[4,8,128,2048]{2,3,1,0:T(8,128)(2,1)}, s32[4,8,256]{2,1,0:T(8,128)S(1)}, bf16[4,8,256]{2,1,0:T(8,128)(2,1)S(1)}, /*index=5*/s32[]{:T(128)}, s32[]{:T(128)}) while((s32[]{:T(128)}, f32[128,256]{1,0:T(8,128)S(1)}, bf16[4,8,128,2048]{2,3,1,0:T(8,128)(2,1)}, ...), condition=%wide.region_5.6_spmd.clone, body=%wide.region_4.5_spmd.clone.sunk | while | flops 1082195968 | bytes 12882027 | solution.py:94
  321.4 2.6 fusion.109
  324.1 3.2 fusion.110
  329.9 3.2 fusion.110
  335.6 3.2 fusion.110
  341.3 3.2 fusion.110
  344.5 37.4 %reduce-scatter.2.cloned.1.call-done = f32[128,256]{1,0:T(8,128)} async-done(((f32[2048,256]{1,0:T(8,128)}), f32[128,256]{1,0:T(8,128)}) %reduce-scatter.2.cloned.1.call-update) | async-done | bytes 131088 | tf_op jit(solution)/shard_map/reduce_scatter | solution.py:100
  (73 shorter events, 17.5 us)
Async XLA Ops:
  6.5 70.9 %copy-start = (bf16[32]{0:T(256)(128)(2,1)S(1)}, bf16[32]{0:T(256)(128)(2,1)}, u32[]{:S(2)}) copy-start(bf16[32]{0:T(256)(128)(2,1)} %param.19) | copy-start | bytes 196
  8.5 30.7 %copy-start.1 = (bf16[128,256]{1,0:T(8,128)(2,1)}, bf16[128,256]{1,0:T(8,128)(2,1)S(1)}, u32[]{:S(2)}) copy-start(bf16[128,256]{1,0:T(8,128)(2,1)S(1)} %multiply_multiply_fusion) | copy-start | bytes 196612
  52.9 5.5 %copy-start.2 = (bf16[32,32]{1,0:T(8,128)(2,1)S(1)}, bf16[32,32]{1,0:T(8,128)(2,1)}, u32[]{:S(2)}) copy-start(bf16[32,32]{1,0:T(8,128)(2,1)} %param.18) | copy-start | bytes 6148
  52.9 5.5 %copy-start.3 = (s32[32]{0:T(128)S(1)}, s32[32]{0:T(128)}, u32[]{:S(2)}) copy-start(s32[32]{0:T(128)} %param.17) | copy-start | bytes 388
  70.6 228.3 %all-to-all-start = ((bf16[8,32,128,256]{3,2,1,0:T(8,128)(2,1)}), bf16[8,32,128,256]{3,2,1,0:T(8,128)(2,1)}, u32[]{:S(2)}, u32[]{:S(2)}) async-start(bf16[8,32,128,256]{3,2,1,0:T(8,128)(2,1)} %stack.2), calls=%async_computation | async-start | bytes 33554432 | tf_op jit(solution)/shard_map/all_to_all | solution.py:84
  76.4 122.2 %all-gather.2.cloned.1.call-start = ((), (), s32[]{:S(2)}) async-start(), calls=%async_computation.2 | async-start | bytes 1114112 | tf_op jit(solution)/shard_map/all_gather | solution.py:63
  77.1 304.8 %reduce-scatter.2.cloned.1.call-start = ((), (), s32[]{:S(2)}) async-start(), calls=%async_computation.3 | async-start | bytes 2228224 | tf_op jit(solution)/shard_map/reduce_scatter | solution.py:100
Sparse Core Ops, SparseCore 0:
  79.6 118.9 all-gather.1
  246.4 135.4 reduce-scatter.1
